TPU v7x, 16 devices: a whole 2x2x2 slice. The times are simulated.
16 devices in a mesh: dp: 16 (over z, y, x, core).
Axes of the slice: x: 2, y: 2, z: 2, core: 2. Of those that a mesh axis runs over, the one named last changes fastest.
Arguments:
- hidden: bfloat16 [32768, 6144], P('dp')
- router_w: bfloat16 [6144, 160], replicated
- expert_idx: int32 [32768, 8], P('dp')
- gate_grad: float32 [32768, 8], P('dp')
Outputs:
- output 1: float32 [32768, 8], P('dp')
- output 2: float32 [], replicated
- output 3: bfloat16 [32768, 6144], P('dp')
- output 4: float32 [6144, 160], replicated
All inputs are finite; a program needn't handle non-finite values.
Results may differ from a plain program's by a relative error of at most 0.0078759.
Values sent between devices are 32-bit elements.
A program may use at most 1 GiB of HBM per device.

v0:
```python
import jax
import jax.numpy as jnp
from jax import lax
from jax.sharding import PartitionSpec as P

LOSS_ALPHA = 0.001


def gate_forward(hidden, router_w, expert_idx):
    logits = jnp.dot(hidden, router_w, preferred_element_type=jnp.float32)
    router_probs = jax.nn.softmax(logits, axis=-1)
    expert_ids = jnp.arange(router_w.shape[1], dtype=jnp.int32)
    idx_hits = expert_idx[:, :, None] == expert_ids[None, None, :]
    picked = jnp.sum(jnp.where(idx_hits, router_probs[:, None, :], 0.0), axis=2)
    pick_sum = jnp.sum(picked, axis=1, keepdims=True)
    return router_probs, idx_hits, pick_sum, picked / pick_sum


def logit_backward(router_probs, idx_hits, pick_sum, gate_probs, gate_grad, expert_freq, loss_scale, total_rows):
    num_experts = router_probs.shape[1]
    scaled_grad = loss_scale * gate_grad
    pick_grad = (scaled_grad - jnp.sum(scaled_grad * gate_probs, axis=1, keepdims=True)) / pick_sum
    aux_coef = loss_scale * LOSS_ALPHA * num_experts / total_rows
    prob_grad = jnp.sum(jnp.where(idx_hits, pick_grad[:, :, None], 0.0), axis=1) + aux_coef * expert_freq[None, :]
    logit_grad = router_probs * (prob_grad - jnp.sum(router_probs * prob_grad, axis=1, keepdims=True))
    return logit_grad.astype(jnp.bfloat16)


def solution(mesh):
    group_size = mesh.shape["dp"]

    def device_step(hidden, router_w, expert_idx, gate_grad):
        total_rows = hidden.shape[0] * group_size
        num_experts = router_w.shape[1]
        loss_scale = float(total_rows * num_experts * num_experts)
        router_probs, idx_hits, pick_sum, gate_probs = gate_forward(hidden, router_w, expert_idx)
        local_counts = jnp.sum(idx_hits, axis=(0, 1), dtype=jnp.float32)
        expert_freq = lax.psum(local_counts, "dp") / total_rows
        prob_mean = lax.psum(jnp.sum(router_probs, axis=0), "dp") / total_rows
        aux_loss = LOSS_ALPHA * num_experts * jnp.sum(expert_freq * prob_mean)
        grad_bf = logit_backward(router_probs, idx_hits, pick_sum, gate_probs, gate_grad, expert_freq, loss_scale, total_rows)
        hidden_grad = lax.dot_general(grad_bf, router_w, (((1,), (1,)), ((), ())), preferred_element_type=jnp.float32).astype(jnp.bfloat16)
        router_part = lax.dot_general(hidden, grad_bf, (((0,), (0,)), ((), ())), preferred_element_type=jnp.float32)
        router_grad = lax.psum(router_part, "dp")
        return gate_probs, aux_loss, hidden_grad, router_grad

    return jax.shard_map(device_step, mesh=mesh, in_specs=(P("dp", None), P(None, None), P("dp", None), P("dp", None)), out_specs=(P("dp", None), P(), P("dp", None), P(None, None)), check_vma=False)
```

profile of v0, /device:TPU:0, one launch (start us, length us, event | category | flops | bytes accessed | tf_op | source)
XLA Modules:
  0.0 170.9 jit_solution(9975352337223916031)
XLA Ops:
  7.2 0.0 copy-start
  7.2 0.0 all-reduce.2.cloned.1.call-start
  7.2 1.5 copy-done
  8.7 13.2 %fusion.2 = (f32[2048]{0:T(1024)S(1)}, f32[2048,160]{0,1:T(8,128)S(1)}) fusion(bf16[2048,6144]{1,0:T(8,128)(2,1)} %param.4, bf16[6144,160]{0,1:T(8,128)(2,1)S(1)} %copy-done), kind=kOutput, calls=%fused_computation.17 | convolution fusion | flops 4026857472 | bytes 28450816 | tf_op jit(solution)/shard_map/dot_general | solution.py:10
  21.9 0.2 fusion.1
  22.1 0.0 copy-start.4
  22.1 0.2 fusion
  22.3 0.6 copy-done.4
  23.0 1.9 %select_reduce_fusion = (f32[2048]{0:T(1024)S(1)}, f32[2048,8]{0,1:T(8,128)S(1)}) fusion(f32[2048,160]{0,1:T(8,128)S(1)} %fusion, s32[2048,8]{0,1:T(8,128)S(1)} %copy-done.4), kind=kLoop, calls=%fused_computation.1 | loop fusion | flops 10467328 | bytes 1449984 | tf_op jit(solution)/shard_map/reduce_sum | solution.py:15
  24.8 0.6 multiply_reduce_fusion.1
  25.5 4.3 %select_reduce_fusion.2 = (f32[2048,160]{0,1:T(8,128)}, f32[160]{0:T(256)S(1)}) fusion(f32[2048,8]{0,1:T(8,128)S(1)} %subtract_divide_fusion, s32[2048,8]{0,1:T(8,128)S(1)} %copy-done.4), kind=kLoop, calls=%fused_computation.3 | loop fusion | flops 15400800 | bytes 1442432 | tf_op jit(solution)/shard_map/reduce_sum | solution.py:24
  29.8 34.8 %psum.21 = f32[160]{0:T(256)S(1)} all-reduce(f32[160]{0:T(256)S(1)} %get-tuple-element.9), channel_id=1, replica_groups=mesh['dp'=16] {'dp'}, use_global_device_ids=true, to_apply=%region_5.6 | all-reduce | flops 160 | bytes 1280 | tf_op jit(solution)/shard_map/psum | solution.py:38
  64.5 1.8 %multiply_reduce_fusion = (f32[2048]{0:T(1024)S(1)}, f32[160]{0:T(256)S(1)}) fusion(f32[2048,160]{0,1:T(8,128)} %get-tuple-element.8, f32[160]{0:T(256)S(1)} %broadcast_multiply_fusion, f32[2048]{0:T(1024)S(1)} %fusion.1, f32[2048,160]{0,1:T(8,128)S(1)} %get-tuple-element.13, f32[2048]{0:T(1024)S(1)} %get-tuple-element.12), kind=kLoop, calls=%fused_computation.8 | loop fusion | flops 1963872 | bytes 2647296 | tf_op jit(solution)/shard_map/reduce_sum | solution.py:25
  66.4 0.0 copy-done.1
  66.4 0.4 multiply_convert_fusion
  66.8 0.0 copy-start.2
  66.8 0.8 copy-done.2
  67.6 12.3 %convolution_bitcast_fusion = f32[6144,160]{0,1:T(8,128)} fusion(bf16[2048,160]{0,1:T(8,128)(2,1)S(1)} %multiply_convert_fusion, bf16[2048,6144]{1,0:T(8,128)(2,1)} %param.4), kind=kOutput, calls=%fused_computation.6 | convolution fusion | flops 4026531840 | bytes 29753344 | tf_op jit(solution)/shard_map/dot_general | solution.py:43
  79.9 0.0 all-reduce.2.cloned.1.call-update
  80.0 33.2 %psum.22 = f32[160]{0:T(256)S(1)} all-reduce(f32[160]{0:T(256)S(1)} %get-tuple-element.7), channel_id=1, replica_groups=mesh['dp'=16] {'dp'}, use_global_device_ids=true, to_apply=%region_7.8 | all-reduce | flops 160 | bytes 1280 | tf_op jit(solution)/shard_map/psum | solution.py:39
  113.1 0.6 multiply_reduce_fusion.2
  114.4 12.4 %convolution_convert_fusion = bf16[2048,6144]{1,0:T(8,128)(2,1)} fusion(bf16[2048,160]{0,1:T(8,128)(2,1)S(1)} %copy-done.3, bf16[6144,160]{0,1:T(8,128)(2,1)S(1)} %copy-done), kind=kOutput, calls=%fused_computation | convolution fusion | flops 4039114752 | bytes 27787264 | tf_op jit(solution)/shard_map/dot_general | solution.py:42
  126.8 31.7 %all-reduce.2.cloned.1.call-done = f32[6144,160]{0,1:T(8,128)} async-done(((f32[6144,160]{0,1:T(8,128)}), f32[6144,160]{0,1:T(8,128)}) %all-reduce.2.cloned.1.call-update) | async-done | bytes 3932176 | tf_op jit(solution)/shard_map/psum | solution.py:44
  158.5 4.4 %copy.12 = f32[6144,160]{0,1:T(8,128)} copy(f32[6144,160]{0,1:T(8,128)} %all-reduce.2.cloned.1.call-done) | data formatting | bytes 7864320
  (7 shorter events, 0.0 us)
Async XLA Ops:
  7.2 1.6 copy-start
  7.2 151.3 %all-reduce.2.cloned.1.call-start = ((), (), s32[]{:S(2)}) async-start(), calls=%async_computation | async-start | bytes 7864320 | tf_op jit(solution)/shard_map/psum | solution.py:44
  22.1 0.8 copy-start.4
  23.0 1.9 %copy-start.5 = (f32[2048,8]{0,1:T(8,128)S(1)}, f32[2048,8]{0,1:T(8,128)}, u32[]{:S(2)}) copy-start(f32[2048,8]{0,1:T(8,128)} %param.7) | copy-start | bytes 196612
  64.5 1.8 %copy-start.1 = (f32[2048,160]{0,1:T(8,128)S(1)}, f32[2048,160]{0,1:T(8,128)}, u32[]{:S(2)}) copy-start(f32[2048,160]{0,1:T(8,128)} %get-tuple-element.8) | copy-start | bytes 3932164
  66.8 0.8 copy-start.2
  79.9 34.5 %copy-start.3 = (bf16[2048,160]{0,1:T(8,128)(2,1)S(1)}, bf16[2048,160]{0,1:T(8,128)(2,1)}, u32[]{:S(2)}) copy-start(bf16[2048,160]{0,1:T(8,128)(2,1)} %copy-done.2) | copy-start | bytes 1966084
Sparse Core Ops, SparseCore 0:
  80.1 78.3 all-reduce.1
where the time goes:
time: 171 us
  blocking collectives  67.9 us (40%)
  matrix products  38 us (22%)
  waiting for transfers between devices  31.7 us (19%)
  between operations  15.9 us (9%)
  other arithmetic  9.98 us (6%)
  local copies, waits for them, and re-layouts  7.39 us (4%)
    psum x1, blocking collectives, device_step(): expert_freq = lax.psum(local_counts, 'dp') / total_rows  34.8 us
    psum x1, blocking collectives, device_step(): prob_mean = lax.psum(jnp.sum(router_probs, axis=0), 'dp') / total_rows  33.2 us
    psum x1, waiting for transfers between devices, device_step(): router_grad = lax.psum(router_part, 'dp')  31.7 us
    dot_general x1, matrix products, gate_forward(): logits = jnp.dot(hidden, router_w, preferred_element_type=jnp.float32)  13.2 us
    dot_general x1, matrix products, device_step(): lax.dot_general(grad_bf, router_w, (((1,), (1,)), ((), ())), preferred_el...  12.4 us
    dot_general x1, matrix products, device_step(): lax.dot_general(hidden, grad_bf, (((0,), (0,)), ((), ())), preferred_elem...  12.3 us
    unnamed x13, local copies, waits for them, and re-layouts  7.39 us
    reduce_sum x1, other arithmetic, logit_backward(): jnp.sum(jnp.where(idx_hits, pick_grad[:, :, None], 0.0), axis=1)  4.26 us
  transfers between devices with their start and end apart: 1, of which 1 were waited for; matrix products, arithmetic and copies ran while one was open for 8% of the time, Pallas kernels for 0%

commit v1 on v0

v1 whole, which is shorter than its diff:
```python
import functools

import jax
import jax.numpy as jnp
from jax import lax
from jax.experimental import pallas as pl
from jax.experimental.pallas import tpu as pltpu
from jax.sharding import PartitionSpec as P

LOSS_ALPHA = 0.001
MESH = pl.DeviceIdType.MESH
TB = 512
SLAB = 256
LAG = 2
ANY = pl.BlockSpec(memory_space=pl.ANY)
VMEM = pl.BlockSpec(memory_space=pltpu.VMEM)


def first_kernel(total_rows, num_devices, hid_hbm, wt_hbm, idx_ref, gg_ref,
                 gt_ref, gates_ref, aux_ref, out_ref,
                 hid, wt, probs, pgrad, psum, flane, cnts, auxs, part, dbuf, rx,
                 hsem, wsem, csend, crecv, asend, arecv, dsend, drecv, xsend, xrecv, gsend, grecv, esend, erecv):
    tokens, width = hid.shape
    experts = wt.shape[0]
    half = experts // 2
    nblk = tokens // TB
    loss_scale = float(total_rows * experts * experts)
    aux_coef = loss_scale * LOSS_ALPHA * experts / total_rows

    me = lax.axis_index("dp")
    core, bx, by, bz = me % 2, (me // 2) % 2, (me // 4) % 2, me // 8
    partner = me + 1 - 2 * core
    across = {"x": me + 2 - 4 * bx, "y": me + 4 - 8 * by, "z": me + 8 - 16 * bz}
    bits = {"x": bx, "y": by, "z": bz}
    routes = (("x", "y", "z"), ("y", "z", "x"), ("z", "x", "y"))
    mine = pl.ds(pl.multiple_of(core * half, 8), half)
    theirs = pl.ds(pl.multiple_of((1 - core) * half, 8), half)

    def hid_copy(b):
        rows = pl.ds(pl.multiple_of(b * TB, TB), TB)
        return pltpu.make_async_copy(hid_hbm.at[rows], hid.at[rows], hsem.at[b])

    w_copy = pltpu.make_async_copy(wt_hbm, wt, wsem)
    w_copy.start()
    for b in range(nblk):
        hid_copy(b).start()

    barrier = pltpu.get_barrier_semaphore()
    for d in range(1, num_devices):
        pl.semaphore_signal(barrier, inc=1, device_id=((me + d) % num_devices,), device_id_type=MESH)

    erows = cnts.shape[2]
    eids = lax.broadcasted_iota(jnp.int32, (erows, 128), 0)

    def count(i, acc):
        ids = idx_ref[:, pl.ds(pl.multiple_of(i * 128, 128), 128)]
        for j in range(ids.shape[0]):
            acc = acc + jnp.where(eids == ids[j:j + 1, :], 1.0, 0.0)
        return acc

    local = lax.fori_loop(0, tokens // 128, count, jnp.zeros((erows, 128), jnp.float32))
    row = jnp.sum(local.T, axis=0, keepdims=True)
    cnts[0] = jnp.broadcast_to(row, (8, erows))
    pl.semaphore_wait(barrier, num_devices - 1)

    def spread(buf, send, recv):
        copies = []
        for d in range(1, num_devices):
            copies.append(pltpu.make_async_remote_copy(
                buf.at[0], buf.at[d], send.at[d], recv.at[d],
                device_id=((me + d) % num_devices,), device_id_type=MESH))
        for c in copies:
            c.start()
        return copies

    count_copies = spread(cnts, csend, crecv)
    psum[...] = jnp.zeros_like(psum)
    w_copy.wait()

    def cols(b):
        return pl.ds(pl.multiple_of(b * TB, TB), TB)

    def logits(b):
        hid_copy(b).wait()
        rows = cols(b)
        probs[:, rows] = lax.dot_general(wt[...], hid[rows, :], (((1,), (1,)), ((), ())),
                                         preferred_element_type=jnp.float32)

    ids_e = lax.broadcasted_iota(jnp.int32, (experts, TB), 0)

    def forward(b):
        c = cols(b)
        lg = probs[:, c]
        ex = jnp.exp(lg - jnp.max(lg, axis=0, keepdims=True))
        p = ex / jnp.sum(ex, axis=0, keepdims=True)
        probs[:, c] = p
        ids = idx_ref[:, c]
        picked = jnp.concatenate(
            [jnp.sum(jnp.where(ids_e == ids[j:j + 1, :], p, 0.0), axis=0, keepdims=True)
             for j in range(ids.shape[0])], axis=0)
        pick_sum = jnp.sum(picked, axis=0, keepdims=True)
        gates = picked / pick_sum
        gates_ref[:, c] = gates
        sg = loss_scale * gg_ref[:, c]
        pgrad[:, c] = (sg - jnp.sum(sg * gates, axis=0, keepdims=True)) / pick_sum
        acc = p[:, 0:128]
        for i in range(1, TB // 128):
            acc = acc + p[:, i * 128:(i + 1) * 128]
        psum[...] += acc

    def backward(b):
        c = cols(b)
        p = probs[:, c]
        ids = idx_ref[:, c]
        pg = pgrad[:, c]
        f = flane[...]
        prob_grad = jnp.zeros_like(p)
        for j in range(ids.shape[0]):
            prob_grad = jnp.where(ids_e == ids[j:j + 1, :], pg[j:j + 1, :], prob_grad)
        prob_grad = prob_grad + aux_coef * jnp.concatenate([f] * (TB // 128), axis=1)
        inner = jnp.sum(p * prob_grad, axis=0, keepdims=True)
        gt_ref[:, c] = (p * (prob_grad - inner)).astype(jnp.bfloat16)

    logits(0)
    for b in range(1, nblk):
        logits(b)
        forward(b - 1)
        if b == nblk - 2:
            for cp in count_copies:
                cp.wait()
            tot = cnts[0]
            for d in range(1, num_devices):
                tot = tot + cnts[d]
            freq = tot[0:1, :] / total_rows
            flane[...] = jnp.broadcast_to(freq, (128, erows)).T[:experts, :]
            for bb in range(b):
                backward(bb)
        elif b > nblk - 2:
            backward(b - 1)
    forward(nblk - 1)
    backward(nblk - 1)

    def slab(p, k):
        flips = ((7 - k) // 4, ((7 - k) // 2) % 2, (7 - k) % 2)
        v = {}
        for name, fl in zip(routes[p], flips):
            v[name] = 1 - bits[name] if fl else bits[name]
        return p * 8 + v["z"] * 4 + v["y"] * 2 + v["x"]

    def dcopy(p, k):
        s = slab(p, k)
        return pltpu.make_async_remote_copy(part.at[s, theirs], dbuf.at[p * 8 + k], dsend.at[p * 8 + k],
                                            drecv.at[p * 8 + k], device_id=(partner,), device_id_type=MESH)

    def xcopy(p, k):
        to = across[routes[p][0 if k < 4 else 1 if k < 6 else 2]]
        return pltpu.make_async_remote_copy(part.at[slab(p, k), mine], rx.at[p * 7 + k], xsend.at[p * 7 + k],
                                            xrecv.at[p * 7 + k], device_id=(to,), device_id_type=MESH)

    def gcopy(p, k, dim):
        s = slab(p, k)
        j = k - (4, 2, 1)[dim]
        return pltpu.make_async_remote_copy(out_ref.at[s, mine], out_ref.at[s, mine], gsend.at[p * 7 + j],
                                            grecv.at[p * 7 + j], device_id=(across[routes[p][dim]],),
                                            device_id_type=MESH)

    def ecopy(p, k):
        s = slab(p, k)
        return pltpu.make_async_remote_copy(out_ref.at[s, mine], out_ref.at[s, mine], esend.at[p * 8 + k],
                                            erecv.at[p * 8 + k], device_id=(partner,), device_id_type=MESH)

    def compute(p, k):
        s = slab(p, k)
        part[s] = jnp.dot(gt_ref[...], hid[:, pl.ds(pl.multiple_of(s * SLAB, SLAB), SLAB)],
                          preferred_element_type=jnp.float32)
        dcopy(p, k).start()

    def reduce_first(k):
        for p in range(3):
            s = slab(p, k)
            dcopy(p, k).wait_recv()
            part[s, mine] = part[s, mine] + dbuf[p * 8 + k]
            if k < 4:
                xcopy(p, k).start()

    for k in range(8):
        for p in range(3):
            compute(p, k)
        if k >= LAG:
            reduce_first(k - LAG)
        if k == 2:
            auxs[0] = jnp.broadcast_to(jnp.sum(psum[...] * flane[...]), (8, 128))
            aux_copies = spread(auxs, asend, arecv)
    for k in range(8 - LAG, 8):
        reduce_first(k)

    for k in (4, 5, 6):
        for p in range(3):
            s = slab(p, k)
            xcopy(p, k - 4).wait_recv()
            acc = part[s, mine] + rx[p * 7 + k - 4]
            if k == 6:
                xcopy(p, 4).wait_recv()
                acc = acc + rx[p * 7 + 4]
            part[s, mine] = acc
            xcopy(p, k).start()
    for p in range(3):
        s = slab(p, 7)
        for i in (3, 5, 6):
            xcopy(p, i).wait_recv()
        out_ref[s, mine] = part[s, mine] + rx[p * 7 + 3] + rx[p * 7 + 5] + rx[p * 7 + 6]
        for dim in (2, 1, 0):
            gcopy(p, 7, dim).start()
        ecopy(p, 7).start()
    for k in (6, 5, 4, 3, 2, 1, 0):
        for p in range(3):
            gcopy(p, k + (1 if k == 6 else 2 if k >= 4 else 4), 2 if k == 6 else 1 if k >= 4 else 0).wait_recv()
            if k == 6:
                gcopy(p, 6, 1).start()
            if k >= 4:
                gcopy(p, k, 0).start()
            ecopy(p, k).start()

    for cp in aux_copies:
        cp.wait()
    tot = auxs[0]
    for d in range(1, num_devices):
        tot = tot + auxs[d]
    aux_ref[...] = tot * (LOSS_ALPHA * experts / total_rows)

    for k in range(8):
        for p in range(3):
            dcopy(p, k).wait_send()
            if k < 7:
                xcopy(p, k).wait_send()
            ecopy(p, k).wait()
    for p in range(3):
        for k, dims in ((7, (0, 1, 2)), (6, (0, 1)), (5, (0,)), (4, (0,))):
            for dim in dims:
                gcopy(p, k, dim).wait_send()


def second_kernel(gt_ref, wt_ref, gates_in, aux_in, rg_in, hg_ref, gates_out, aux_out, rg_out, g_scr, sems):
    i = pl.program_id(0)
    rows = hg_ref.shape[0]
    slabs = rg_in.shape[0]
    others = [pltpu.make_async_copy(gates_in, gates_out, sems.at[slabs]),
              pltpu.make_async_copy(aux_in.at[pl.ds(0, 1)], aux_out, sems.at[slabs + 1])]
    others += [pltpu.make_async_copy(rg_in.at[s], rg_out.at[:, pl.ds(s * SLAB, SLAB)], sems.at[s])
               for s in range(slabs)]

    @pl.when(i == 0)
    def _():
        for c in others:
            c.start()

    g = gt_ref[:, pl.ds(pl.multiple_of(i * rows, rows), rows)].T
    hg_ref[...] = jnp.dot(g, wt_ref[...], preferred_element_type=jnp.float32).astype(jnp.bfloat16)

    @pl.when(i == pl.num_programs(0) - 1)
    def _():
        for c in others:
            c.wait()


def solution(mesh):
    n = mesh.shape["dp"]

    def device_step(hidden, router_w, expert_idx, gate_grad):
        tokens, width = hidden.shape
        experts = router_w.shape[1]
        top_k = expert_idx.shape[1]
        slabs = width // SLAB
        half = experts // 2
        f32 = jnp.float32
        wt = router_w.T
        gt, gates, aux, rg = pl.pallas_call(
            functools.partial(first_kernel, tokens * n, n),
            out_shape=(jax.ShapeDtypeStruct((experts, tokens), jnp.bfloat16),
                       jax.ShapeDtypeStruct((top_k, tokens), f32),
                       jax.ShapeDtypeStruct((8, 128), f32),
                       jax.ShapeDtypeStruct((slabs, experts, SLAB), f32)),
            in_specs=[ANY, ANY, VMEM, VMEM],
            out_specs=(VMEM, VMEM, VMEM, VMEM),
            scratch_shapes=[
                pltpu.VMEM((tokens, width), jnp.bfloat16),
                pltpu.VMEM((experts, width), jnp.bfloat16),
                pltpu.VMEM((experts, tokens), f32),
                pltpu.VMEM((top_k, tokens), f32),
                pltpu.VMEM((experts, 128), f32),
                pltpu.VMEM((experts, 128), f32),
                pltpu.VMEM((n, 8, 256), f32),
                pltpu.VMEM((n, 8, 128), f32),
                pltpu.VMEM((slabs, experts, SLAB), f32),
                pltpu.VMEM((slabs, half, SLAB), f32),
                pltpu.VMEM((21, half, SLAB), f32),
                pltpu.SemaphoreType.DMA((tokens // TB,)),
                pltpu.SemaphoreType.DMA,
                pltpu.SemaphoreType.DMA((n,)), pltpu.SemaphoreType.DMA((n,)),
                pltpu.SemaphoreType.DMA((n,)), pltpu.SemaphoreType.DMA((n,)),
                pltpu.SemaphoreType.DMA((24,)), pltpu.SemaphoreType.DMA((24,)),
                pltpu.SemaphoreType.DMA((21,)), pltpu.SemaphoreType.DMA((21,)),
                pltpu.SemaphoreType.DMA((21,)), pltpu.SemaphoreType.DMA((21,)),
                pltpu.SemaphoreType.DMA((24,)), pltpu.SemaphoreType.DMA((24,)),
            ],
            compiler_params=pltpu.CompilerParams(collective_id=0, has_side_effects=True,
                                                 vmem_limit_bytes=40 * 2 ** 20),
        )(hidden, wt, expert_idx.T, gate_grad.T)
        rows = 256
        hg, gates, aux, rg = pl.pallas_call(
            second_kernel,
            grid=(tokens // rows,),
            out_shape=(jax.ShapeDtypeStruct((tokens, width), jnp.bfloat16),
                       jax.ShapeDtypeStruct((top_k, tokens), f32),
                       jax.ShapeDtypeStruct((1, 128), f32),
                       jax.ShapeDtypeStruct((experts, width), f32)),
            in_specs=[VMEM, VMEM, ANY, ANY, ANY],
            out_specs=(pl.BlockSpec((rows, width), lambda i: (i, 0)), ANY, ANY, ANY),
            scratch_shapes=[pltpu.VMEM((8, 128), jnp.bfloat16), pltpu.SemaphoreType.DMA((slabs + 2,))],
            compiler_params=pltpu.CompilerParams(vmem_limit_bytes=40 * 2 ** 20),
        )(gt, wt, gates, aux, rg)
        return gates.T, aux[0, 0], hg, rg.T

    return jax.shard_map(device_step, mesh=mesh,
                         in_specs=(P("dp", None), P(None, None), P("dp", None), P("dp", None)),
                         out_specs=(P("dp", None), P(), P("dp", None), P(None, None)), check_vma=False)
```

time: 171 us -> 76.1 us (0.45)
  Pallas kernels: 0 us -> 71.8 us
  blocking collectives: 67.9 us -> 0 us
  matrix products: 38 us -> 0 us
  waiting for transfers between devices: 31.7 us -> 0 us
  between operations: 15.9 us -> 0.81 us
  other arithmetic: 9.98 us -> 0 us
  local copies, waits for them, and re-layouts: 7.39 us -> 3.22 us
    pallas_call x0 -> x2, Pallas kernels: none -> 71.8 us  [the longest x1 58.9 us: device_step(): pl.pallas_call(functools.partial(first_kernel, tokens * n, n), out_shape=...]
    psum x2 -> x0, blocking collectives: 67.9 us -> none  [the longest x1 34.8 us: device_step(): expert_freq = lax.psum(local_counts, 'dp') / total_rows]
    dot_general x3 -> x0, matrix products: 38 us -> none  [the longest x1 13.2 us: gate_forward(): logits = jnp.dot(hidden, router_w, preferred_element_type=jnp.float32)]
    psum x1 -> x0, waiting for transfers between devices: 31.7 us -> none  [device_step(): router_grad = lax.psum(router_part, 'dp')]
    reduce_sum x6 -> x0, other arithmetic: 9.4 us -> none  [the longest x1 4.26 us: logit_backward(): jnp.sum(jnp.where(idx_hits, pick_grad[:, :, None], 0.0), axis=1)]
    unnamed x13 -> x6, local copies, waits for them, and re-layouts: 7.39 us -> 3.22 us
  transfers between devices with their start and end apart: 1 -> 0, of which waited for: 1 -> 0; matrix products, arithmetic and copies ran while one was open for 8% -> 0% of each run, Pallas kernels for 0% -> 0%
where the time goes in v1:
time: 76.1 us; the launch traced here: 75.9 us
  Pallas kernels  71.8 us (94%)
  local copies, waits for them, and re-layouts  3.22 us (4%)
  between operations  0.81 us (1%)
    pallas_call x1, Pallas kernels, device_step(): pl.pallas_call(functools.partial(first_kernel, tokens * n, n), out_shape=...  58.9 us
    pallas_call x1, Pallas kernels, device_step(): pl.pallas_call(second_kernel, grid=(tokens // rows,), out_shape=(jax.Shap...  12.9 us
    unnamed x6, local copies, waits for them, and re-layouts  3.22 us

profile of v1, /device:TPU:0, one launch (start us, length us, event | category | flops | bytes accessed | tf_op | source)
XLA Modules:
  0.0 75.9 jit_solution(12504844385217428377)
XLA Ops:
  0.6 0.0 copy-start
  0.6 1.5 %copy-done = bf16[6144,160]{0,1:T(8,128)(2,1)S(1)} copy-done((bf16[6144,160]{0,1:T(8,128)(2,1)S(1)}, bf16[6144,160]{0,1:T(8,128)(2,1)}, u32[]{:S(2)}) %copy-start) | copy-done | bytes 1966104
  2.2 0.0 copy-start.1
  2.2 0.8 %copy-done.1 = s32[2048,8]{0,1:T(8,128)S(1)} copy-done((s32[2048,8]{0,1:T(8,128)S(1)}, s32[2048,8]{0,1:T(8,128)}, u32[]{:S(2)}) %copy-start.1) | copy-done | bytes 65560
  3.0 0.0 copy-start.2
  3.0 0.8 %copy-done.2 = f32[2048,8]{0,1:T(8,128)S(1)} copy-done((f32[2048,8]{0,1:T(8,128)S(1)}, f32[2048,8]{0,1:T(8,128)}, u32[]{:S(2)}) %copy-start.2) | copy-done | bytes 65560
  3.9 58.9 %shard_map.75 = (bf16[160,2048]{1,0:T(8,128)(2,1)S(1)}, f32[8,2048]{1,0:T(8,128)S(1)}, f32[8,128]{1,0:T(8,128)S(1)}, f32[24,160,256]{2,1,0:T(8,128)S(1)}) custom-call(bf16[2048,6144]{1,0:T(8,128)(2,1)} %hid_hbm.1, bf16[160,6144]{1,0:T(8,128)(2,1)S(1)} %bitcast.7, s32[8,2048]{1,0:T(8,128)S(1)} %bitcast.9, f32[8,2048]{1,0:T(8,128)S(1)} %bitcast.10), custom_call_target="tpu_custom_call" | custom-call | tf_op jit(solution)/shard_map/pallas_call | solution.py:277
  62.8 12.9 %shard_map.76 = (bf16[2048,6144]{1,0:T(8,128)(2,1)}, f32[8,2048]{1,0:T(8,128)}, f32[1,128]{1,0:T(1,128)}, f32[160,6144]{1,0:T(8,128)}) custom-call(bf16[160,2048]{1,0:T(8,128)(2,1)S(1)} %get-tuple-element.12.gt_ref, bf16[160,6144]{1,0:T(8,128)(2,1)S(1)} %bitcast.8, f32[8,2048]{1,0:T(8,128)S(1)} %get-tuple-element.13.gates_in, ...), custom_call_target="tpu_custom_call" | custom-call | tf_op jit(solution)/shard_map/pallas_call | solution.py:310
Async XLA Ops:
  0.6 1.5 %copy-start = (bf16[6144,160]{0,1:T(8,128)(2,1)S(1)}, bf16[6144,160]{0,1:T(8,128)(2,1)}, u32[]{:S(2)}) copy-start(bf16[6144,160]{0,1:T(8,128)(2,1)} %param.5) | copy-start | bytes 5898244
  2.2 0.8 %copy-start.1 = (s32[2048,8]{0,1:T(8,128)S(1)}, s32[2048,8]{0,1:T(8,128)}, u32[]{:S(2)}) copy-start(s32[2048,8]{0,1:T(8,128)} %param.6) | copy-start | bytes 196612
  3.0 0.8 %copy-start.2 = (f32[2048,8]{0,1:T(8,128)S(1)}, f32[2048,8]{0,1:T(8,128)}, u32[]{:S(2)}) copy-start(f32[2048,8]{0,1:T(8,128)} %param.7) | copy-start | bytes 196612

commit v2 on v0

v2 whole, which is shorter than its diff:
```python
import functools

import jax
import jax.numpy as jnp
from jax import lax
from jax.experimental import pallas as pl
from jax.experimental.pallas import tpu as pltpu
from jax.sharding import PartitionSpec as P

LOSS_ALPHA = 0.001
MESH = pl.DeviceIdType.MESH
TB = 256
LANES = 128
SLAB = 256
LAG = 2
FLIGHT = 4
READY = 5
HBM = pl.BlockSpec(memory_space=pltpu.HBM)
VMEM = pl.BlockSpec(memory_space=pltpu.VMEM)


def loop(lo, hi, fn):
    def step(i, carry):
        fn(i)
        return carry

    lax.fori_loop(lo, hi, step, 0)


def first_kernel(total_rows, num_devices, hid_hbm, wt_hbm, idx_hbm, gg_hbm,
                 gt_ref, gates_ref, aux_ref, out_ref, wt,
                 idx_ref, gg_ref, hid, wn, probs, pgrad, psum, flane, cnts, auxs, part, dbuf, rx,
                 isem, hsem, wsem, csem, asem, dsend, drecv, xsend, xrecv, gsend, grecv, esem):
    tokens, width = hid.shape
    experts = wt.shape[0]
    half = experts // 2
    nblk = tokens // TB
    loss_scale = float(total_rows * experts * experts)
    aux_coef = loss_scale * LOSS_ALPHA * experts / total_rows

    me = lax.axis_index("dp")
    core, bx, by, bz = me % 2, (me // 2) % 2, (me // 4) % 2, me // 8
    partner = me + 1 - 2 * core
    across = {"x": me + 2 - 4 * bx, "y": me + 4 - 8 * by, "z": me + 8 - 16 * bz}
    bits = {"x": bx, "y": by, "z": bz}
    routes = (("x", "y", "z"), ("y", "z", "x"), ("z", "x", "y"))
    mine = pl.ds(pl.multiple_of(core * half, 8), half)
    theirs = pl.ds(pl.multiple_of((1 - core) * half, 8), half)

    def hid_copy(b):
        rows = pl.ds(pl.multiple_of(b * TB, TB), TB)
        return pltpu.make_async_copy(hid_hbm.at[rows], hid.at[rows], hsem.at[b])

    def remote(src, dst, send, recv, to):
        return pltpu.make_async_remote_copy(src, dst, send, recv, device_id=(to,), device_id_type=MESH)

    idx_copy = pltpu.make_async_copy(idx_hbm, idx_ref, isem.at[0])
    gg_copy = pltpu.make_async_copy(gg_hbm, gg_ref, isem.at[1])
    w_copy = pltpu.make_async_copy(wt_hbm, wt, wsem)
    idx_copy.start()
    w_copy.start()
    gg_copy.start()
    for b in range(FLIGHT):
        hid_copy(b).start()

    barrier = pltpu.get_barrier_semaphore()
    loop(1, num_devices, lambda d: pl.semaphore_signal(
        barrier, inc=1, device_id=((me + d) % num_devices,), device_id_type=MESH))

    erows = cnts.shape[2]
    eids = lax.broadcasted_iota(jnp.int32, (experts, LANES), 0)

    def count(i, acc):
        ids = idx_ref[:, pl.ds(pl.multiple_of(i * LANES, LANES), LANES)]
        for j in range(ids.shape[0]):
            acc = acc + jnp.where(eids == ids[j:j + 1, :], 1.0, 0.0)
        return acc

    idx_copy.wait()
    local = lax.fori_loop(0, tokens // LANES, count, jnp.zeros((experts, LANES), jnp.float32))
    local = jnp.concatenate([local, jnp.zeros((erows - experts, LANES), jnp.float32)], axis=0)
    row = jnp.sum(local.T, axis=0, keepdims=True)
    cnts[0] = jnp.broadcast_to(row, (8, erows))
    psum[...] = jnp.zeros_like(psum)
    probs[:, pl.ds(tokens - TB, TB)] = jnp.zeros((experts, TB), jnp.float32)
    pl.semaphore_wait(barrier, num_devices - 1)

    def spread(buf, sem):
        loop(1, num_devices, lambda d: remote(
            buf.at[0], buf.at[d], sem.at[0], sem.at[1], (me + d) % num_devices).start())

    def gather_sum(buf, sem):
        rest = buf.at[pl.ds(1, num_devices - 1)]
        remote(rest, rest, sem.at[0], sem.at[1], partner).wait()
        tot = buf[0]
        for d in range(1, num_devices):
            tot = tot + buf[d]
        return tot

    spread(cnts, csem)
    gg_copy.wait()
    w_copy.wait()

    def turn(i):
        c = pl.ds(pl.multiple_of(i * SLAB, SLAB), SLAB)
        wn[c, :] = wt[:, c].T

    loop(0, width // SLAB, turn)

    def logits(b):
        rows = pl.ds(pl.multiple_of(b * TB, TB), TB)
        lg = jnp.dot(hid[rows, :], wn[...], preferred_element_type=jnp.float32)
        probs[:, rows] = lg.T

    groups = range(0, experts, 8)
    base = lax.broadcasted_iota(jnp.int32, (8, LANES), 0)

    def spread_rows(x):
        return [jnp.broadcast_to(x[j:j + 1, :], (8, LANES)) for j in range(x.shape[0])]

    def lanes(i):
        return pl.ds(pl.multiple_of(i * LANES, LANES), LANES)

    def forward_chunk(i):
        c = lanes(i)
        ids = [i - base for i in spread_rows(idx_ref[:, c])]
        top = probs[0:8, c]
        for g in groups[1:]:
            top = jnp.maximum(top, probs[g:g + 8, c])
        top = jnp.max(top, axis=0, keepdims=True)
        total = jnp.zeros((8, LANES), jnp.float32)
        hits = [jnp.zeros((8, LANES), jnp.float32) for _ in ids]
        for g in groups:
            ex = jnp.exp(probs[g:g + 8, c] - top)
            probs[g:g + 8, c] = ex
            total = total + ex
            for j, i in enumerate(ids):
                hits[j] = jnp.where(i == g, ex, hits[j])
        scale = 1.0 / jnp.sum(total, axis=0, keepdims=True)
        picked = jnp.concatenate([jnp.sum(h, axis=0, keepdims=True) for h in hits], axis=0) * scale
        pick_sum = jnp.sum(picked, axis=0, keepdims=True)
        gates = picked / pick_sum
        gates_ref[:, c] = gates
        sg = loss_scale * gg_ref[:, c]
        pgrad[:, c] = (sg - jnp.sum(sg * gates, axis=0, keepdims=True)) / pick_sum
        for g in groups:
            probs[g:g + 8, c] = probs[g:g + 8, c] * scale

    def backward_chunk(i):
        c = lanes(i)
        ids = [i - base for i in spread_rows(idx_ref[:, c])]
        pg = spread_rows(pgrad[:, c])
        inner = jnp.zeros((8, LANES), jnp.float32)
        grads = []
        for g in groups:
            q = jnp.zeros((8, LANES), jnp.float32)
            for j, i in enumerate(ids):
                q = jnp.where(i == g, pg[j], q)
            q = q + aux_coef * flane[g:g + 8, :]
            grads.append(q)
            p = probs[g:g + 8, c]
            psum[g:g + 8, :] += p
            inner = inner + p * q
        inner = jnp.sum(inner, axis=0, keepdims=True)
        for n in range(0, len(grads), 2):
            g = groups[n]
            lo = probs[g:g + 8, c] * (grads[n] - inner)
            hi = probs[g + 8:g + 16, c] * (grads[n + 1] - inner)
            gt_ref[g:g + 16, c] = jnp.concatenate([lo, hi], axis=0).astype(jnp.bfloat16)

    per = TB // LANES

    def arrive(b):
        hid_copy(b).wait()

        @pl.when(b + FLIGHT < nblk)
        def _():
            hid_copy(b + FLIGHT).start()

    def early(b):
        arrive(b)
        logits(b)
        last = (b + nblk - 1) % nblk
        for i in range(per):
            forward_chunk(last * per + i)

    def late(b):
        arrive(b)
        logits(b)
        for i in range(per):
            forward_chunk((b - 1) * per + i)
        for i in range(2 * per):
            backward_chunk((b - READY) * 2 * per + i)

    loop(0, READY, early)
    freq = gather_sum(cnts, csem)[0:1, :] / total_rows
    flane[...] = jnp.broadcast_to(freq, (LANES, erows)).T[:experts, :]
    loop(READY, nblk, late)
    loop((nblk - 1) * per, nblk * per, forward_chunk)
    loop((nblk - READY) * 2 * per, nblk * per, backward_chunk)

    def slab(p, k):
        far = 7 - k
        flips = (far // 4, (far // 2) % 2, far % 2)
        v = {name: bits[name] + fl - 2 * bits[name] * fl for name, fl in zip(routes[p], flips)}
        return p * 8 + v["z"] * 4 + v["y"] * 2 + v["x"]

    def dcopy(p, k):
        return remote(part.at[slab(p, k), theirs], dbuf.at[p * 8 + k], dsend, drecv.at[p * 8 + k], partner)

    def xcopy(p, k, dim):
        return remote(part.at[slab(p, k), mine], rx.at[p * 7 + k], xsend, xrecv.at[p * 7 + k],
                      across[routes[p][dim]])

    def gcopy(p, k, dim):
        s = slab(p, k)
        return remote(out_ref.at[s, mine], out_ref.at[s, mine], gsend, grecv.at[p * 7 + k - (4, 2, 1)[dim]],
                      across[routes[p][dim]])

    def ecopy(p, k):
        s = slab(p, k)
        return remote(out_ref.at[s, mine], out_ref.at[s, mine], esem.at[0], esem.at[1], partner)

    def compute(k):
        for p in range(3):
            s = slab(p, k)
            part[s] = jnp.dot(gt_ref[...], hid[:, pl.ds(pl.multiple_of(s * SLAB, SLAB), SLAB)],
                              preferred_element_type=jnp.float32)
        for p in range(3):
            dcopy(p, k).start()

    def pair_sum(k):
        for p in range(3):
            dcopy(p, k).wait_recv()
            s = slab(p, k)
            part[s, mine] = part[s, mine] + dbuf[p * 8 + k]

    def pair_send(k):
        pair_sum(k)
        for p in range(3):
            xcopy(p, k, 0).start()

    def compute_and_send(k):
        compute(k)
        pair_send(k - LAG)

    loop(0, LAG, compute)
    loop(LAG, 4 + LAG, compute_and_send)
    loop(4 + LAG, 8, compute)
    auxs[0] = jnp.broadcast_to(jnp.sum(psum[...] * flane[...]), (8, 128))
    spread(auxs, asem)
    loop(4, 8, pair_sum)

    def second(k):
        for p in range(3):
            xcopy(p, k - 4, 0).wait_recv()
            s = slab(p, k)
            part[s, mine] = part[s, mine] + rx[p * 7 + k - 4]
            xcopy(p, k, 1).start()

    loop(4, 6, second)
    for p in range(3):
        xcopy(p, 2, 0).wait_recv()
        xcopy(p, 4, 1).wait_recv()
        s = slab(p, 6)
        part[s, mine] = part[s, mine] + rx[p * 7 + 2] + rx[p * 7 + 4]
        xcopy(p, 6, 2).start()
    for p in range(3):
        xcopy(p, 3, 0).wait_recv()
        xcopy(p, 5, 1).wait_recv()
        xcopy(p, 6, 2).wait_recv()
        s = slab(p, 7)
        out_ref[s, mine] = part[s, mine] + rx[p * 7 + 3] + rx[p * 7 + 5] + rx[p * 7 + 6]
        for dim in (2, 1, 0):
            gcopy(p, 7, dim).start()
        ecopy(p, 7).start()
    for p in range(3):
        gcopy(p, 7, 2).wait_recv()
        gcopy(p, 6, 1).start()
        gcopy(p, 6, 0).start()
        ecopy(p, 6).start()

    def relay(i):
        k = 5 - i
        for p in range(3):
            gcopy(p, k + 2, 1).wait_recv()
            gcopy(p, k, 0).start()
            ecopy(p, k).start()

    def close(i):
        k = 3 - i
        for p in range(3):
            gcopy(p, k + 4, 0).wait_recv()
            ecopy(p, k).start()

    loop(0, 2, relay)
    loop(0, 4, close)
    aux_ref[...] = gather_sum(auxs, asem) * (LOSS_ALPHA * experts / total_rows)
    remote(dbuf, dbuf, dsend, drecv.at[0], partner).wait_send()
    remote(rx, rx, xsend, xrecv.at[0], partner).wait_send()
    remote(rx, rx, gsend, grecv.at[0], partner).wait_send()
    remote(dbuf, dbuf, esem.at[0], esem.at[1], partner).wait()


def second_kernel(blocks, gt_ref, wt_ref, gates_in, aux_in, rg_in, hg_ref, gates_out, aux_out, rg_out,
                  buf, sems, rsem, bsems):
    slabs = rg_in.shape[0]
    small = [pltpu.make_async_copy(gates_in, gates_out, sems.at[0]),
             pltpu.make_async_copy(aux_in.at[pl.ds(0, 1)], aux_out, sems.at[1])]
    for c in small:
        c.start()
    loop(0, slabs, lambda s: pltpu.make_async_copy(
        rg_in.at[s], rg_out.at[:, pl.ds(pl.multiple_of(s * SLAB, SLAB), SLAB)], rsem).start())
    start, sem = 0, 0
    for rows, times in blocks:
        def block(i, rows=rows, start=start, sem=sem):
            r = pl.ds(pl.multiple_of(start + i * rows, rows), rows)
            buf[r, :] = jnp.dot(gt_ref[:, r].T, wt_ref[...], preferred_element_type=jnp.float32).astype(jnp.bfloat16)
            pltpu.make_async_copy(buf.at[r], hg_ref.at[r], bsems.at[sem + i]).start()

        loop(0, times, block)
        start, sem = start + rows * times, sem + times
    for c in small:
        c.wait()
    pltpu.make_async_copy(rg_in, rg_in, rsem).wait()
    start, sem = 0, 0
    for rows, times in blocks:
        def wait(i, rows=rows, start=start, sem=sem):
            r = pl.ds(pl.multiple_of(start + i * rows, rows), rows)
            pltpu.make_async_copy(buf.at[r], hg_ref.at[r], bsems.at[sem + i]).wait()

        loop(0, times, wait)
        start, sem = start + rows * times, sem + times


def solution(mesh):
    n = mesh.shape["dp"]

    def device_step(hidden, router_w, expert_idx, gate_grad):
        tokens, width = hidden.shape
        experts = router_w.shape[1]
        top_k = expert_idx.shape[1]
        slabs = width // SLAB
        half = experts // 2
        f32 = jnp.float32
        dma = pltpu.SemaphoreType.DMA
        gt, gates, aux, rg, wt = pl.pallas_call(
            functools.partial(first_kernel, tokens * n, n),
            out_shape=(jax.ShapeDtypeStruct((experts, tokens), jnp.bfloat16),
                       jax.ShapeDtypeStruct((top_k, tokens), f32),
                       jax.ShapeDtypeStruct((8, 128), f32),
                       jax.ShapeDtypeStruct((slabs, experts, SLAB), f32),
                       jax.ShapeDtypeStruct((experts, width), jnp.bfloat16)),
            in_specs=[HBM] * 4,
            out_specs=(VMEM,) * 5,
            scratch_shapes=[
                pltpu.VMEM((top_k, tokens), jnp.int32),
                pltpu.VMEM((top_k, tokens), f32),
                pltpu.VMEM((tokens, width), jnp.bfloat16),
                pltpu.VMEM((width, experts), jnp.bfloat16),
                pltpu.VMEM((experts, tokens), f32),
                pltpu.VMEM((top_k, tokens), f32),
                pltpu.VMEM((experts, 128), f32),
                pltpu.VMEM((experts, 128), f32),
                pltpu.VMEM((n, 8, 256), f32),
                pltpu.VMEM((n, 8, 128), f32),
                pltpu.VMEM((slabs, experts, SLAB), f32),
                pltpu.VMEM((slabs, half, SLAB), f32),
                pltpu.VMEM((21, half, SLAB), f32),
                dma((2,)), dma((tokens // TB,)), dma,
                dma((2,)), dma((2,)),
                dma, dma((24,)), dma, dma((21,)), dma, dma((21,)), dma((2,)),
            ],
            compiler_params=pltpu.CompilerParams(collective_id=0, has_side_effects=True,
                                                 vmem_limit_bytes=40 * 2 ** 20),
        )(hidden, *(pltpu.with_memory_space_constraint(a, pltpu.HBM)
                    for a in (router_w.T, expert_idx.T, gate_grad.T)))
        blocks = [(256, tokens // 256 - 1), (128, 2)]
        hg, gates, aux, rg = pl.pallas_call(
            functools.partial(second_kernel, blocks),
            out_shape=(jax.ShapeDtypeStruct((tokens, width), jnp.bfloat16),
                       jax.ShapeDtypeStruct((top_k, tokens), f32),
                       jax.ShapeDtypeStruct((1, 128), f32),
                       jax.ShapeDtypeStruct((experts, width), f32)),
            in_specs=[VMEM] * 5,
            out_specs=(HBM,) * 4,
            scratch_shapes=[pltpu.VMEM((tokens, width), jnp.bfloat16), dma((2,)), dma,
                            dma((sum(t for _, t in blocks),))],
            compiler_params=pltpu.CompilerParams(vmem_limit_bytes=40 * 2 ** 20),
        )(gt, wt, gates, aux, rg)
        return gates.T, aux[0, 0], hg, rg.T

    return jax.shard_map(device_step, mesh=mesh,
                         in_specs=(P("dp", None), P(None, None), P("dp", None), P("dp", None)),
                         out_specs=(P("dp", None), P(), P("dp", None), P(None, None)), check_vma=False)
```

time: 171 us -> 65.9 us (0.39)
  blocking collectives: 67.9 us -> 0 us
  Pallas kernels: 0 us -> 65.1 us
  matrix products: 38 us -> 0 us
  waiting for transfers between devices: 31.7 us -> 0 us
  between operations: 15.9 us -> 0.64 us
  other arithmetic: 9.98 us -> 0 us
  local copies, waits for them, and re-layouts: 7.39 us -> 0 us
    psum x2 -> x0, blocking collectives: 67.9 us -> none  [the longest x1 34.8 us: device_step(): expert_freq = lax.psum(local_counts, 'dp') / total_rows]
    pallas_call x0 -> x2, Pallas kernels: none -> 65.1 us  [the longest x1 55.2 us: device_step(): pl.pallas_call(functools.partial(first_kernel, tokens * n, n), out_shape=...]
    dot_general x3 -> x0, matrix products: 38 us -> none  [the longest x1 13.2 us: gate_forward(): logits = jnp.dot(hidden, router_w, preferred_element_type=jnp.float32)]
    psum x1 -> x0, waiting for transfers between devices: 31.7 us -> none  [device_step(): router_grad = lax.psum(router_part, 'dp')]
    reduce_sum x6 -> x0, other arithmetic: 9.4 us -> none  [the longest x1 4.26 us: logit_backward(): jnp.sum(jnp.where(idx_hits, pick_grad[:, :, None], 0.0), axis=1)]
    unnamed x13 -> x0, local copies, waits for them, and re-layouts: 7.39 us -> none
  transfers between devices with their start and end apart: 1 -> 0, of which waited for: 1 -> 0; matrix products, arithmetic and copies ran while one was open for 8% -> 0% of each run, Pallas kernels for 0% -> 0%
where the time goes in v2:
time: 65.9 us; the launch traced here: 65.8 us
  Pallas kernels  65.1 us (99%)
    pallas_call x1, Pallas kernels, device_step(): pl.pallas_call(functools.partial(first_kernel, tokens * n, n), out_shape=...  55.2 us
    pallas_call x1, Pallas kernels, device_step(): pl.pallas_call(functools.partial(second_kernel, blocks), out_shape=(jax.S...  9.94 us

profile of v2, /device:TPU:0, one launch (start us, length us, event | category | flops | bytes accessed | tf_op | source)
XLA Modules:
  0.0 65.8 jit_solution(6431299855956141056)
XLA Ops:
  0.6 55.2 %shard_map.75 = (bf16[160,2048]{1,0:T(8,128)(2,1)S(1)}, f32[8,2048]{1,0:T(8,128)S(1)}, f32[8,128]{1,0:T(8,128)S(1)}, f32[24,160,256]{2,1,0:T(8,128)S(1)}, bf16[160,6144]{1,0:T(8,128)(2,1)S(1)}) custom-call(bf16[2048,6144]{1,0:T(8,128)(2,1)} %hid_hbm.1, bf16[160,6144]{1,0:T(8,128)(2,1)} %bitcast.7, s32[8,2048]{1,0:T(8,128)} %bitcast.8, f32[8,2048]{1,0:T(8,128)} %bitcast.9), custom_call_target="tpu_custom_call" | custom-call | tf_op jit(solution)/shard_map/pallas_call | solution.py:347
  55.8 9.9 %shard_map.76 = (bf16[2048,6144]{1,0:T(8,128)(2,1)}, f32[8,2048]{1,0:T(8,128)}, f32[1,128]{1,0:T(1,128)}, f32[160,6144]{1,0:T(8,128)}) custom-call(bf16[160,2048]{1,0:T(8,128)(2,1)S(1)} %get-tuple-element.13.gt_ref, bf16[160,6144]{1,0:T(8,128)(2,1)S(1)} %get-tuple-element.14.wt_ref, f32[8,2048]{1,0:T(8,128)S(1)} %get-tuple-element.15.gates_in, ...), custom_call_target="tpu_custom_call" | custom-call | tf_op jit(solution)/shard_map/pallas_call | solution.py:379

commit v3 on v2

--- a/solution.py
+++ b/solution.py
@@ -9,12 +9,12 @@
 
 LOSS_ALPHA = 0.001
 MESH = pl.DeviceIdType.MESH
-TB = 256
+TB = 512
+COPY = 256
 LANES = 128
 SLAB = 256
 LAG = 2
-FLIGHT = 4
-READY = 5
+FLIGHT = 3
 HBM = pl.BlockSpec(memory_space=pltpu.HBM)
 VMEM = pl.BlockSpec(memory_space=pltpu.VMEM)
 
@@ -29,7 +29,7 @@
 
 def first_kernel(total_rows, num_devices, hid_hbm, wt_hbm, idx_hbm, gg_hbm,
                  gt_ref, gates_ref, aux_ref, out_ref, wt,
-                 idx_ref, gg_ref, hid, wn, probs, pgrad, psum, flane, cnts, auxs, part, dbuf, rx,
+                 idx_ref, gg_ref, hid, probs, pgrad, psum, flane, cnts, auxs, part, dbuf, rx,
                  isem, hsem, wsem, csem, asem, dsend, drecv, xsend, xrecv, gsend, grecv, esem):
     tokens, width = hid.shape
     experts = wt.shape[0]
@@ -48,7 +48,7 @@
     theirs = pl.ds(pl.multiple_of((1 - core) * half, 8), half)
 
     def hid_copy(b):
-        rows = pl.ds(pl.multiple_of(b * TB, TB), TB)
+        rows = pl.ds(pl.multiple_of(b * COPY, COPY), COPY)
         return pltpu.make_async_copy(hid_hbm.at[rows], hid.at[rows], hsem.at[b])
 
     def remote(src, dst, send, recv, to):
@@ -68,17 +68,28 @@
         barrier, inc=1, device_id=((me + d) % num_devices,), device_id_type=MESH))
 
     erows = cnts.shape[2]
-    eids = lax.broadcasted_iota(jnp.int32, (experts, LANES), 0)
+    groups = range(0, experts, 8)
+    base = lax.broadcasted_iota(jnp.int32, (8, LANES), 0)
+
+    def spread_rows(x):
+        return [jnp.broadcast_to(x[j:j + 1, :], (8, LANES)) for j in range(x.shape[0])]
+
+    def lanes(i):
+        return pl.ds(pl.multiple_of(i * LANES, LANES), LANES)
 
     def count(i, acc):
-        ids = idx_ref[:, pl.ds(pl.multiple_of(i * LANES, LANES), LANES)]
-        for j in range(ids.shape[0]):
-            acc = acc + jnp.where(eids == ids[j:j + 1, :], 1.0, 0.0)
-        return acc
+        ids = [i - base for i in spread_rows(idx_ref[:, lanes(i)])]
+        out = []
+        for a, g in zip(acc, groups):
+            for j in ids:
+                a = jnp.where(j == g, a + 1.0, a)
+            out.append(a)
+        return tuple(out)
 
     idx_copy.wait()
-    local = lax.fori_loop(0, tokens // LANES, count, jnp.zeros((experts, LANES), jnp.float32))
-    local = jnp.concatenate([local, jnp.zeros((erows - experts, LANES), jnp.float32)], axis=0)
+    zero = jnp.zeros((8, LANES), jnp.float32)
+    local = lax.fori_loop(0, tokens // LANES, count, (zero,) * len(groups))
+    local = jnp.concatenate(list(local) + [zero] * ((erows - experts) // 8), axis=0)
     row = jnp.sum(local.T, axis=0, keepdims=True)
     cnts[0] = jnp.broadcast_to(row, (8, erows))
     psum[...] = jnp.zeros_like(psum)
@@ -87,39 +98,24 @@
 
     def spread(buf, sem):
         loop(1, num_devices, lambda d: remote(
-            buf.at[0], buf.at[d], sem.at[0], sem.at[1], (me + d) % num_devices).start())
+            buf.at[0, pl.ds(0, 1)], buf.at[d, pl.ds(0, 1)], sem.at[0], sem.at[1], (me + d) % num_devices).start())
 
     def gather_sum(buf, sem):
-        rest = buf.at[pl.ds(1, num_devices - 1)]
+        rest = buf.at[pl.ds(1, num_devices - 1), pl.ds(0, 1)]
         remote(rest, rest, sem.at[0], sem.at[1], partner).wait()
-        tot = buf[0]
+        tot = buf[0, 0:1]
         for d in range(1, num_devices):
-            tot = tot + buf[d]
+            tot = tot + buf[d, 0:1]
         return tot
 
     spread(cnts, csem)
     gg_copy.wait()
     w_copy.wait()
 
-    def turn(i):
-        c = pl.ds(pl.multiple_of(i * SLAB, SLAB), SLAB)
-        wn[c, :] = wt[:, c].T
-
-    loop(0, width // SLAB, turn)
-
     def logits(b):
         rows = pl.ds(pl.multiple_of(b * TB, TB), TB)
-        lg = jnp.dot(hid[rows, :], wn[...], preferred_element_type=jnp.float32)
+        lg = lax.dot_general(hid[rows, :], wt[...], (((1,), (1,)), ((), ())), preferred_element_type=jnp.float32)
         probs[:, rows] = lg.T
-
-    groups = range(0, experts, 8)
-    base = lax.broadcasted_iota(jnp.int32, (8, LANES), 0)
-
-    def spread_rows(x):
-        return [jnp.broadcast_to(x[j:j + 1, :], (8, LANES)) for j in range(x.shape[0])]
-
-    def lanes(i):
-        return pl.ds(pl.multiple_of(i * LANES, LANES), LANES)
 
     def forward_chunk(i):
         c = lanes(i)
@@ -156,7 +152,7 @@
             q = jnp.zeros((8, LANES), jnp.float32)
             for j, i in enumerate(ids):
                 q = jnp.where(i == g, pg[j], q)
-            q = q + aux_coef * flane[g:g + 8, :]
+            q = q + flane[g:g + 8, :]
             grads.append(q)
             p = probs[g:g + 8, c]
             psum[g:g + 8, :] += p
@@ -170,34 +166,30 @@
 
     per = TB // LANES
 
+    ncopy = tokens // COPY
+
     def arrive(b):
-        hid_copy(b).wait()
-
-        @pl.when(b + FLIGHT < nblk)
-        def _():
-            hid_copy(b + FLIGHT).start()
-
-    def early(b):
+        for i in range(TB // COPY):
+            hid_copy(b * (TB // COPY) + i).wait()
+        for i in range(TB // COPY):
+            nxt = b * (TB // COPY) + i + FLIGHT
+
+            @pl.when(nxt < ncopy)
+            def _():
+                hid_copy(nxt).start()
+
+    def block(b):
         arrive(b)
         logits(b)
         last = (b + nblk - 1) % nblk
         for i in range(per):
             forward_chunk(last * per + i)
 
-    def late(b):
-        arrive(b)
-        logits(b)
-        for i in range(per):
-            forward_chunk((b - 1) * per + i)
-        for i in range(2 * per):
-            backward_chunk((b - READY) * 2 * per + i)
-
-    loop(0, READY, early)
-    freq = gather_sum(cnts, csem)[0:1, :] / total_rows
+    loop(0, nblk, block)
+    loop((nblk - 1) * per, nblk * per, forward_chunk)
+    freq = gather_sum(cnts, csem) * (aux_coef / total_rows)
     flane[...] = jnp.broadcast_to(freq, (LANES, erows)).T[:experts, :]
-    loop(READY, nblk, late)
-    loop((nblk - 1) * per, nblk * per, forward_chunk)
-    loop((nblk - READY) * 2 * per, nblk * per, backward_chunk)
+    loop(0, nblk * per, backward_chunk)
 
     def slab(p, k):
         far = 7 - k
@@ -235,21 +227,23 @@
             s = slab(p, k)
             part[s, mine] = part[s, mine] + dbuf[p * 8 + k]
 
-    def pair_send(k):
-        pair_sum(k)
-        for p in range(3):
-            xcopy(p, k, 0).start()
+        @pl.when(k < 4)
+        def _():
+            for p in range(3):
+                xcopy(p, k, 0).start()
 
     def compute_and_send(k):
-        compute(k)
-        pair_send(k - LAG)
-
-    loop(0, LAG, compute)
-    loop(LAG, 4 + LAG, compute_and_send)
-    loop(4 + LAG, 8, compute)
+        @pl.when(k >= LAG)
+        def _():
+            pair_sum(k - LAG)
+
+        @pl.when(k < 8)
+        def _():
+            compute(k)
+
+    loop(0, 8 + LAG, compute_and_send)
     auxs[0] = jnp.broadcast_to(jnp.sum(psum[...] * flane[...]), (8, 128))
     spread(auxs, asem)
-    loop(4, 8, pair_sum)
 
     def second(k):
         for p in range(3):
@@ -271,8 +265,11 @@
         xcopy(p, 6, 2).wait_recv()
         s = slab(p, 7)
         out_ref[s, mine] = part[s, mine] + rx[p * 7 + 3] + rx[p * 7 + 5] + rx[p * 7 + 6]
-        for dim in (2, 1, 0):
+        gcopy(p, 7, 2).start()
+    for dim in (1, 0):
+        for p in range(3):
             gcopy(p, 7, dim).start()
+    for p in range(3):
         ecopy(p, 7).start()
     for p in range(3):
         gcopy(p, 7, 2).wait_recv()
@@ -295,7 +292,7 @@
 
     loop(0, 2, relay)
     loop(0, 4, close)
-    aux_ref[...] = gather_sum(auxs, asem) * (LOSS_ALPHA * experts / total_rows)
+    aux_ref[...] = jnp.broadcast_to(gather_sum(auxs, asem) / loss_scale, aux_ref.shape)
     remote(dbuf, dbuf, dsend, drecv.at[0], partner).wait_send()
     remote(rx, rx, xsend, xrecv.at[0], partner).wait_send()
     remote(rx, rx, gsend, grecv.at[0], partner).wait_send()
@@ -357,7 +354,6 @@
                 pltpu.VMEM((top_k, tokens), jnp.int32),
                 pltpu.VMEM((top_k, tokens), f32),
                 pltpu.VMEM((tokens, width), jnp.bfloat16),
-                pltpu.VMEM((width, experts), jnp.bfloat16),
                 pltpu.VMEM((experts, tokens), f32),
                 pltpu.VMEM((top_k, tokens), f32),
                 pltpu.VMEM((experts, 128), f32),
@@ -367,7 +363,7 @@
                 pltpu.VMEM((slabs, experts, SLAB), f32),
                 pltpu.VMEM((slabs, half, SLAB), f32),
                 pltpu.VMEM((21, half, SLAB), f32),
-                dma((2,)), dma((tokens // TB,)), dma,
+                dma((2,)), dma((tokens // COPY,)), dma,
                 dma((2,)), dma((2,)),
                 dma, dma((24,)), dma, dma((21,)), dma, dma((21,)), dma((2,)),
             ],

time: 65.9 us -> 61.3 us (0.930)
  Pallas kernels: 65.1 us -> 60.5 us
    pallas_call x1, Pallas kernels: 55.2 us -> 50.5 us  [device_step(): pl.pallas_call(functools.partial(first_kernel, tokens * n, n), out_shape=...]
where the time goes in v3:
time: 61.3 us; the launch traced here: 61.1 us
  Pallas kernels  60.5 us (99%)
  between operations  0.64 us (1%)
    pallas_call x1, Pallas kernels, device_step(): pl.pallas_call(functools.partial(first_kernel, tokens * n, n), out_shape=...  50.5 us
    pallas_call x1, Pallas kernels, device_step(): pl.pallas_call(functools.partial(second_kernel, blocks), out_shape=(jax.S...  9.95 us

profile of v3, /device:TPU:0, one launch (start us, length us, event | category | flops | bytes accessed | tf_op | source)
XLA Modules:
  0.0 61.1 jit_solution(14008500895825260774)
XLA Ops:
  0.6 50.5 %shard_map.75 = (bf16[160,2048]{1,0:T(8,128)(2,1)S(1)}, f32[8,2048]{1,0:T(8,128)S(1)}, f32[8,128]{1,0:T(8,128)S(1)}, f32[24,160,256]{2,1,0:T(8,128)S(1)}, bf16[160,6144]{1,0:T(8,128)(2,1)S(1)}) custom-call(bf16[2048,6144]{1,0:T(8,128)(2,1)} %hid_hbm.1, bf16[160,6144]{1,0:T(8,128)(2,1)} %bitcast.7, s32[8,2048]{1,0:T(8,128)} %bitcast.8, f32[8,2048]{1,0:T(8,128)} %bitcast.9), custom_call_target="tpu_custom_call" | custom-call | tf_op jit(solution)/shard_map/pallas_call | solution.py:344
  51.2 9.9 %shard_map.76 = (bf16[2048,6144]{1,0:T(8,128)(2,1)}, f32[8,2048]{1,0:T(8,128)}, f32[1,128]{1,0:T(1,128)}, f32[160,6144]{1,0:T(8,128)}) custom-call(bf16[160,2048]{1,0:T(8,128)(2,1)S(1)} %get-tuple-element.13.gt_ref, bf16[160,6144]{1,0:T(8,128)(2,1)S(1)} %get-tuple-element.14.wt_ref, f32[8,2048]{1,0:T(8,128)S(1)} %get-tuple-element.15.gates_in, ...), custom_call_target="tpu_custom_call" | custom-call | tf_op jit(solution)/shard_map/pallas_call | solution.py:375

commit v4 on v3

--- a/solution.py
+++ b/solution.py
@@ -14,6 +14,8 @@
 LANES = 128
 SLAB = 256
 LAG = 2
+ROWS = 256
+EARLY = 2
 FLIGHT = 3
 HBM = pl.BlockSpec(memory_space=pltpu.HBM)
 VMEM = pl.BlockSpec(memory_space=pltpu.VMEM)
@@ -28,7 +30,7 @@
 
 
 def first_kernel(total_rows, num_devices, hid_hbm, wt_hbm, idx_hbm, gg_hbm,
-                 gt_ref, gates_ref, aux_ref, out_ref, wt,
+                 gt_ref, gates_ref, aux_ref, out_ref, wt, hg_ref,
                  idx_ref, gg_ref, hid, probs, pgrad, psum, flane, cnts, auxs, part, dbuf, rx,
                  isem, hsem, wsem, csem, asem, dsend, drecv, xsend, xrecv, gsend, grecv, esem):
     tokens, width = hid.shape
@@ -41,9 +43,6 @@
     me = lax.axis_index("dp")
     core, bx, by, bz = me % 2, (me // 2) % 2, (me // 4) % 2, me // 8
     partner = me + 1 - 2 * core
-    across = {"x": me + 2 - 4 * bx, "y": me + 4 - 8 * by, "z": me + 8 - 16 * bz}
-    bits = {"x": bx, "y": by, "z": bz}
-    routes = (("x", "y", "z"), ("y", "z", "x"), ("z", "x", "y"))
     mine = pl.ds(pl.multiple_of(core * half, 8), half)
     theirs = pl.ds(pl.multiple_of((1 - core) * half, 8), half)
 
@@ -191,23 +190,33 @@
     flane[...] = jnp.broadcast_to(freq, (LANES, erows)).T[:experts, :]
     loop(0, nblk * per, backward_chunk)
 
+    axis_bits = (bx, by, bz)
+
     def slab(p, k):
         far = 7 - k
-        flips = (far // 4, (far // 2) % 2, far % 2)
-        v = {name: bits[name] + fl - 2 * bits[name] * fl for name, fl in zip(routes[p], flips)}
-        return p * 8 + v["z"] * 4 + v["y"] * 2 + v["x"]
+        s = p * 8
+        for a in range(3):
+            i = (a + 3 - p) % 3
+            flip = (far // ((8 - 5 * i + i * i) // 2)) % 2
+            s = s + (1, 2, 4)[a] * (axis_bits[a] + flip - 2 * axis_bits[a] * flip)
+        return s
+
+    def across(p, dim):
+        a = (p + dim) % 3
+        stride = 2 + a + a * a
+        return me + stride * (1 - 2 * ((me // stride) % 2))
 
     def dcopy(p, k):
         return remote(part.at[slab(p, k), theirs], dbuf.at[p * 8 + k], dsend, drecv.at[p * 8 + k], partner)
 
     def xcopy(p, k, dim):
         return remote(part.at[slab(p, k), mine], rx.at[p * 7 + k], xsend, xrecv.at[p * 7 + k],
-                      across[routes[p][dim]])
+                      across(p, dim))
 
     def gcopy(p, k, dim):
         s = slab(p, k)
         return remote(out_ref.at[s, mine], out_ref.at[s, mine], gsend, grecv.at[p * 7 + k - (4, 2, 1)[dim]],
-                      across[routes[p][dim]])
+                      across(p, dim))
 
     def ecopy(p, k):
         s = slab(p, k)
@@ -232,66 +241,100 @@
             for p in range(3):
                 xcopy(p, k, 0).start()
 
-    def compute_and_send(k):
-        @pl.when(k >= LAG)
-        def _():
-            pair_sum(k - LAG)
-
-        @pl.when(k < 8)
-        def _():
-            compute(k)
-
-    loop(0, 8 + LAG, compute_and_send)
-    auxs[0] = jnp.broadcast_to(jnp.sum(psum[...] * flane[...]), (8, 128))
-    spread(auxs, asem)
-
     def second(k):
-        for p in range(3):
+        def one(p):
             xcopy(p, k - 4, 0).wait_recv()
             s = slab(p, k)
             part[s, mine] = part[s, mine] + rx[p * 7 + k - 4]
             xcopy(p, k, 1).start()
 
-    loop(4, 6, second)
-    for p in range(3):
+        loop(0, 3, one)
+
+    def order(i):
+        return i + ((i + 3) // 4) % 2 * (2 * (i % 2) - 1)
+
+    def compute_and_send(i):
+        @pl.when(i == LAG + 4)
+        def _():
+            second(4)
+
+        @pl.when(i >= LAG)
+        def _():
+            pair_sum(order(i - LAG))
+
+        @pl.when(i < 8)
+        def _():
+            compute(order(i))
+
+    loop(0, 8 + LAG, compute_and_send)
+    second(5)
+
+    def hidden_rows(i):
+        r = pl.ds(pl.multiple_of(i * ROWS, ROWS), ROWS)
+        hg_ref[r, :] = jnp.dot(gt_ref[:, r].T, wt[...], preferred_element_type=jnp.float32).astype(jnp.bfloat16)
+
+    def third(p):
         xcopy(p, 2, 0).wait_recv()
         xcopy(p, 4, 1).wait_recv()
         s = slab(p, 6)
         part[s, mine] = part[s, mine] + rx[p * 7 + 2] + rx[p * 7 + 4]
         xcopy(p, 6, 2).start()
-    for p in range(3):
+
+    loop(0, 3, third)
+    loop(0, EARLY, hidden_rows)
+    auxs[0] = jnp.broadcast_to(jnp.sum(psum[...] * flane[...]), (8, 128))
+    spread(auxs, asem)
+
+    def final(p):
         xcopy(p, 3, 0).wait_recv()
         xcopy(p, 5, 1).wait_recv()
         xcopy(p, 6, 2).wait_recv()
         s = slab(p, 7)
         out_ref[s, mine] = part[s, mine] + rx[p * 7 + 3] + rx[p * 7 + 5] + rx[p * 7 + 6]
         gcopy(p, 7, 2).start()
-    for dim in (1, 0):
-        for p in range(3):
+
+    loop(0, 3, final)
+
+    def own(dim):
+        def one(p):
             gcopy(p, 7, dim).start()
-    for p in range(3):
-        ecopy(p, 7).start()
-    for p in range(3):
+
+        loop(0, 3, one)
+
+    def pair(k):
+        def one(p):
+            ecopy(p, k).start()
+
+        loop(0, 3, one)
+
+    own(1)
+    own(0)
+    pair(7)
+
+    def relay_second(p):
         gcopy(p, 7, 2).wait_recv()
         gcopy(p, 6, 1).start()
+
+    def relay_first(p):
         gcopy(p, 6, 0).start()
         ecopy(p, 6).start()
 
+    loop(0, 3, relay_second)
+    loop(0, 3, relay_first)
+
     def relay(i):
-        k = 5 - i
-        for p in range(3):
-            gcopy(p, k + 2, 1).wait_recv()
-            gcopy(p, k, 0).start()
-            ecopy(p, k).start()
+        k, p = 5 - i // 3, i % 3
+        gcopy(p, k + 2, 1).wait_recv()
+        gcopy(p, k, 0).start()
+        ecopy(p, k).start()
 
     def close(i):
-        k = 3 - i
-        for p in range(3):
-            gcopy(p, k + 4, 0).wait_recv()
-            ecopy(p, k).start()
-
-    loop(0, 2, relay)
-    loop(0, 4, close)
+        k, p = 3 - i // 3, i % 3
+        gcopy(p, k + 4, 0).wait_recv()
+        ecopy(p, k).start()
+
+    loop(0, 6, relay)
+    loop(0, 12, close)
     aux_ref[...] = jnp.broadcast_to(gather_sum(auxs, asem) / loss_scale, aux_ref.shape)
     remote(dbuf, dbuf, dsend, drecv.at[0], partner).wait_send()
     remote(rx, rx, xsend, xrecv.at[0], partner).wait_send()
@@ -299,32 +342,35 @@
     remote(dbuf, dbuf, esem.at[0], esem.at[1], partner).wait()
 
 
-def second_kernel(blocks, gt_ref, wt_ref, gates_in, aux_in, rg_in, hg_ref, gates_out, aux_out, rg_out,
+def second_kernel(blocks, gt_ref, wt_ref, hg_in, gates_in, aux_in, rg_in, hg_ref, gates_out, aux_out, rg_out,
                   buf, sems, rsem, bsems):
     slabs = rg_in.shape[0]
-    small = [pltpu.make_async_copy(gates_in, gates_out, sems.at[0]),
+    early = hg_in.shape[0]
+    small = [pltpu.make_async_copy(hg_in, hg_ref.at[pl.ds(0, early)], sems.at[2]),
+             pltpu.make_async_copy(gates_in, gates_out, sems.at[0]),
              pltpu.make_async_copy(aux_in.at[pl.ds(0, 1)], aux_out, sems.at[1])]
     for c in small:
         c.start()
     loop(0, slabs, lambda s: pltpu.make_async_copy(
         rg_in.at[s], rg_out.at[:, pl.ds(pl.multiple_of(s * SLAB, SLAB), SLAB)], rsem).start())
-    start, sem = 0, 0
+    start, sem = early, 0
     for rows, times in blocks:
         def block(i, rows=rows, start=start, sem=sem):
             r = pl.ds(pl.multiple_of(start + i * rows, rows), rows)
-            buf[r, :] = jnp.dot(gt_ref[:, r].T, wt_ref[...], preferred_element_type=jnp.float32).astype(jnp.bfloat16)
-            pltpu.make_async_copy(buf.at[r], hg_ref.at[r], bsems.at[sem + i]).start()
+            here = pl.ds(pl.multiple_of(start - early + i * rows, rows), rows)
+            buf[here, :] = jnp.dot(gt_ref[:, r].T, wt_ref[...], preferred_element_type=jnp.float32).astype(jnp.bfloat16)
+            pltpu.make_async_copy(buf.at[here], hg_ref.at[r], bsems.at[sem + i]).start()
 
         loop(0, times, block)
         start, sem = start + rows * times, sem + times
     for c in small:
         c.wait()
     pltpu.make_async_copy(rg_in, rg_in, rsem).wait()
-    start, sem = 0, 0
+    start, sem = early, 0
     for rows, times in blocks:
         def wait(i, rows=rows, start=start, sem=sem):
             r = pl.ds(pl.multiple_of(start + i * rows, rows), rows)
-            pltpu.make_async_copy(buf.at[r], hg_ref.at[r], bsems.at[sem + i]).wait()
+            pltpu.make_async_copy(buf.at[pl.ds(0, rows)], hg_ref.at[r], bsems.at[sem + i]).wait()
 
         loop(0, times, wait)
         start, sem = start + rows * times, sem + times
@@ -341,15 +387,16 @@
         half = experts // 2
         f32 = jnp.float32
         dma = pltpu.SemaphoreType.DMA
-        gt, gates, aux, rg, wt = pl.pallas_call(
+        gt, gates, aux, rg, wt, head = pl.pallas_call(
             functools.partial(first_kernel, tokens * n, n),
             out_shape=(jax.ShapeDtypeStruct((experts, tokens), jnp.bfloat16),
                        jax.ShapeDtypeStruct((top_k, tokens), f32),
                        jax.ShapeDtypeStruct((8, 128), f32),
                        jax.ShapeDtypeStruct((slabs, experts, SLAB), f32),
-                       jax.ShapeDtypeStruct((experts, width), jnp.bfloat16)),
+                       jax.ShapeDtypeStruct((experts, width), jnp.bfloat16),
+                       jax.ShapeDtypeStruct((EARLY * ROWS, width), jnp.bfloat16)),
             in_specs=[HBM] * 4,
-            out_specs=(VMEM,) * 5,
+            out_specs=(VMEM,) * 6,
             scratch_shapes=[
                 pltpu.VMEM((top_k, tokens), jnp.int32),
                 pltpu.VMEM((top_k, tokens), f32),
@@ -371,19 +418,20 @@
                                                  vmem_limit_bytes=40 * 2 ** 20),
         )(hidden, *(pltpu.with_memory_space_constraint(a, pltpu.HBM)
                     for a in (router_w.T, expert_idx.T, gate_grad.T)))
-        blocks = [(256, tokens // 256 - 1), (128, 2)]
+        rest = tokens - EARLY * ROWS
+        blocks = [(ROWS, rest // ROWS)]
         hg, gates, aux, rg = pl.pallas_call(
             functools.partial(second_kernel, blocks),
             out_shape=(jax.ShapeDtypeStruct((tokens, width), jnp.bfloat16),
                        jax.ShapeDtypeStruct((top_k, tokens), f32),
                        jax.ShapeDtypeStruct((1, 128), f32),
                        jax.ShapeDtypeStruct((experts, width), f32)),
-            in_specs=[VMEM] * 5,
+            in_specs=[VMEM] * 6,
             out_specs=(HBM,) * 4,
-            scratch_shapes=[pltpu.VMEM((tokens, width), jnp.bfloat16), dma((2,)), dma,
+            scratch_shapes=[pltpu.VMEM((rest, width), jnp.bfloat16), dma((3,)), dma,
                             dma((sum(t for _, t in blocks),))],
             compiler_params=pltpu.CompilerParams(vmem_limit_bytes=40 * 2 ** 20),
-        )(gt, wt, gates, aux, rg)
+        )(gt, wt, head, gates, aux, rg)
         return gates.T, aux[0, 0], hg, rg.T
 
     return jax.shard_map(device_step, mesh=mesh,

time: 61.3 us -> 60.5 us (0.987)
  Pallas kernels: 60.5 us -> 59.8 us
where the time goes in v4:
time: 60.5 us; the launch traced here: 60.4 us
  Pallas kernels  59.8 us (99%)
  between operations  0.64 us (1%)
    pallas_call x1, Pallas kernels, device_step(): pl.pallas_call(functools.partial(first_kernel, tokens * n, n), out_shape=...  50 us
    pallas_call x1, Pallas kernels, device_step(): pl.pallas_call(functools.partial(second_kernel, blocks), out_shape=(jax.S...  9.75 us

profile of v4, /device:TPU:0, one launch (start us, length us, event | category | flops | bytes accessed | tf_op | source)
XLA Modules:
  0.0 60.4 jit_solution(7778099082120981854)
XLA Ops:
  0.6 50.0 %shard_map.75 = (bf16[160,2048]{1,0:T(8,128)(2,1)S(1)}, f32[8,2048]{1,0:T(8,128)S(1)}, f32[8,128]{1,0:T(8,128)S(1)}, f32[24,160,256]{2,1,0:T(8,128)S(1)}, bf16[1...) custom-call(bf16[2048,6144]{1,0:T(8,128)(2,1)} %hid_hbm.1, bf16[160,6144]{1,0:T(8,128)(2,1)} %bitcast.7, ...), custom_call_target="tpu_custom_call" | custom-call | tf_op jit(solution)/shard_map/pallas_call | solution.py:390
  50.7 9.8 %shard_map.76 = (bf16[2048,6144]{1,0:T(8,128)(2,1)}, f32[8,2048]{1,0:T(8,128)}, f32[1,128]{1,0:T(1,128)}, f32[160,6144]{1,0:T(8,128)}) custom-call(bf16[160,2048]{1,0:T(8,128)(2,1)S(1)} %get-tuple-element.14.gt_ref, bf16[160,6144]{1,0:T(8,128)(2,1)S(1)} %get-tuple-element.15.wt_ref, bf16[512,6144]{1,0:T(8,128)(2,1)S(1)} %get-tuple-element.16.hg_in, ...), custom_call_target="tpu_custom_call" | custom-call | tf_op jit(solution)/shard_map/pallas_call | solution.py:423

commit v5 on v4

--- a/solution.py
+++ b/solution.py
@@ -32,7 +32,7 @@
 def first_kernel(total_rows, num_devices, hid_hbm, wt_hbm, idx_hbm, gg_hbm,
                  gt_ref, gates_ref, aux_ref, out_ref, wt, hg_ref,
                  idx_ref, gg_ref, hid, probs, pgrad, psum, flane, cnts, auxs, part, dbuf, rx,
-                 isem, hsem, wsem, csem, asem, dsend, drecv, xsend, xrecv, gsend, grecv, esem):
+                 isem, hsem, wsem, csem, asem, dsend, drecv, xsend, xrecv, gsend, esem):
     tokens, width = hid.shape
     experts = wt.shape[0]
     half = experts // 2
@@ -185,10 +185,18 @@
             forward_chunk(last * per + i)
 
     loop(0, nblk, block)
-    loop((nblk - 1) * per, nblk * per, forward_chunk)
+    def forward_pair(i):
+        forward_chunk(2 * i)
+        forward_chunk(2 * i + 1)
+
+    loop((nblk - 1) * per // 2, nblk * per // 2, forward_pair)
     freq = gather_sum(cnts, csem) * (aux_coef / total_rows)
     flane[...] = jnp.broadcast_to(freq, (LANES, erows)).T[:experts, :]
-    loop(0, nblk * per, backward_chunk)
+    def backward_pair(i):
+        backward_chunk(2 * i)
+        backward_chunk(2 * i + 1)
+
+    loop(0, nblk * per // 2, backward_pair)
 
     axis_bits = (bx, by, bz)
 
@@ -207,15 +215,19 @@
         return me + stride * (1 - 2 * ((me // stride) % 2))
 
     def dcopy(p, k):
-        return remote(part.at[slab(p, k), theirs], dbuf.at[p * 8 + k], dsend, drecv.at[p * 8 + k], partner)
+        return remote(part.at[slab(p, k), theirs], dbuf.at[p * 8 + k], dsend, drecv.at[k], partner)
 
     def xcopy(p, k, dim):
-        return remote(part.at[slab(p, k), mine], rx.at[p * 7 + k], xsend, xrecv.at[p * 7 + k],
-                      across(p, dim))
+        group = k if dim == 0 else 3 if k > 4 else 2
+        return remote(part.at[slab(p, k), mine], rx.at[p * 7 + k], xsend, xrecv.at[group], across(p, dim))
+
+    def arrived(sem, units):
+        ref = rx.at[pl.ds(0, 3 * units)]
+        remote(ref, ref, xsend, sem, partner).wait_recv()
 
     def gcopy(p, k, dim):
         s = slab(p, k)
-        return remote(out_ref.at[s, mine], out_ref.at[s, mine], gsend, grecv.at[p * 7 + k - (4, 2, 1)[dim]],
+        return remote(out_ref.at[s, mine], out_ref.at[s, mine], gsend, drecv.at[k - (4, 2, 1)[dim]],
                       across(p, dim))
 
     def ecopy(p, k):
@@ -231,8 +243,8 @@
             dcopy(p, k).start()
 
     def pair_sum(k):
+        arrived(drecv.at[k], 1)
         for p in range(3):
-            dcopy(p, k).wait_recv()
             s = slab(p, k)
             part[s, mine] = part[s, mine] + dbuf[p * 8 + k]
 
@@ -242,8 +254,9 @@
                 xcopy(p, k, 0).start()
 
     def second(k):
+        arrived(xrecv.at[k - 4], 1)
+
         def one(p):
-            xcopy(p, k - 4, 0).wait_recv()
             s = slab(p, k)
             part[s, mine] = part[s, mine] + rx[p * 7 + k - 4]
             xcopy(p, k, 1).start()
@@ -273,9 +286,9 @@
         r = pl.ds(pl.multiple_of(i * ROWS, ROWS), ROWS)
         hg_ref[r, :] = jnp.dot(gt_ref[:, r].T, wt[...], preferred_element_type=jnp.float32).astype(jnp.bfloat16)
 
+    arrived(xrecv.at[2], 2)
+
     def third(p):
-        xcopy(p, 2, 0).wait_recv()
-        xcopy(p, 4, 1).wait_recv()
         s = slab(p, 6)
         part[s, mine] = part[s, mine] + rx[p * 7 + 2] + rx[p * 7 + 4]
         xcopy(p, 6, 2).start()
@@ -285,60 +298,51 @@
     auxs[0] = jnp.broadcast_to(jnp.sum(psum[...] * flane[...]), (8, 128))
     spread(auxs, asem)
 
+    arrived(xrecv.at[3], 3)
+
     def final(p):
-        xcopy(p, 3, 0).wait_recv()
-        xcopy(p, 5, 1).wait_recv()
-        xcopy(p, 6, 2).wait_recv()
         s = slab(p, 7)
         out_ref[s, mine] = part[s, mine] + rx[p * 7 + 3] + rx[p * 7 + 5] + rx[p * 7 + 6]
         gcopy(p, 7, 2).start()
 
     loop(0, 3, final)
 
-    def own(dim):
-        def one(p):
-            gcopy(p, 7, dim).start()
-
-        loop(0, 3, one)
-
     def pair(k):
         def one(p):
             ecopy(p, k).start()
 
         loop(0, 3, one)
 
-    own(1)
-    own(0)
+
+    def forward_on(k, dim):
+        def one(p):
+            gcopy(p, k, dim).start()
+
+        loop(0, 3, one)
+
+    forward_on(7, 1)
+    forward_on(7, 0)
     pair(7)
-
-    def relay_second(p):
-        gcopy(p, 7, 2).wait_recv()
-        gcopy(p, 6, 1).start()
-
-    def relay_first(p):
-        gcopy(p, 6, 0).start()
-        ecopy(p, 6).start()
-
-    loop(0, 3, relay_second)
-    loop(0, 3, relay_first)
+    arrived(drecv.at[6], 1)
+    forward_on(6, 1)
+    forward_on(6, 0)
+    pair(6)
 
     def relay(i):
-        k, p = 5 - i // 3, i % 3
-        gcopy(p, k + 2, 1).wait_recv()
-        gcopy(p, k, 0).start()
-        ecopy(p, k).start()
+        arrived(drecv.at[5 - i], 1)
+        forward_on(5 - i, 0)
+        pair(5 - i)
 
     def close(i):
-        k, p = 3 - i // 3, i % 3
-        gcopy(p, k + 4, 0).wait_recv()
-        ecopy(p, k).start()
-
-    loop(0, 6, relay)
-    loop(0, 12, close)
+        arrived(drecv.at[3 - i], 1)
+        pair(3 - i)
+
+    loop(0, 2, relay)
+    loop(0, 4, close)
     aux_ref[...] = jnp.broadcast_to(gather_sum(auxs, asem) / loss_scale, aux_ref.shape)
     remote(dbuf, dbuf, dsend, drecv.at[0], partner).wait_send()
     remote(rx, rx, xsend, xrecv.at[0], partner).wait_send()
-    remote(rx, rx, gsend, grecv.at[0], partner).wait_send()
+    remote(rx, rx, gsend, drecv.at[0], partner).wait_send()
     remote(dbuf, dbuf, esem.at[0], esem.at[1], partner).wait()
 
 
@@ -412,7 +416,7 @@
                 pltpu.VMEM((21, half, SLAB), f32),
                 dma((2,)), dma((tokens // COPY,)), dma,
                 dma((2,)), dma((2,)),
-                dma, dma((24,)), dma, dma((21,)), dma, dma((21,)), dma((2,)),
+                dma, dma((8,)), dma, dma((4,)), dma, dma((2,)),
             ],
             compiler_params=pltpu.CompilerParams(collective_id=0, has_side_effects=True,
                                                  vmem_limit_bytes=40 * 2 ** 20),

time: 60.5 us -> 60 us (level)
  no operation moved by 1% of the time
where the time goes in v5:
time: 60 us; the launch traced here: 59.9 us
  Pallas kernels  59.2 us (99%)
  between operations  0.64 us (1%)
    pallas_call x1, Pallas kernels, device_step(): pl.pallas_call(functools.partial(first_kernel, tokens * n, n), out_shape=...  49.5 us
    pallas_call x1, Pallas kernels, device_step(): pl.pallas_call(functools.partial(second_kernel, blocks), out_shape=(jax.S...  9.75 us

profile of v5, /device:TPU:0, one launch (start us, length us, event | category | flops | bytes accessed | tf_op | source)
XLA Modules:
  0.0 59.9 jit_solution(8057047610737783195)
XLA Ops:
  0.6 49.5 %shard_map.75 = (bf16[160,2048]{1,0:T(8,128)(2,1)S(1)}, f32[8,2048]{1,0:T(8,128)S(1)}, f32[8,128]{1,0:T(8,128)S(1)}, f32[24,160,256]{2,1,0:T(8,128)S(1)}, bf16[1...) custom-call(bf16[2048,6144]{1,0:T(8,128)(2,1)} %hid_hbm.1, bf16[160,6144]{1,0:T(8,128)(2,1)} %bitcast.7, ...), custom_call_target="tpu_custom_call" | custom-call | tf_op jit(solution)/shard_map/pallas_call | solution.py:394
  50.1 9.8 %shard_map.76 = (bf16[2048,6144]{1,0:T(8,128)(2,1)}, f32[8,2048]{1,0:T(8,128)}, f32[1,128]{1,0:T(1,128)}, f32[160,6144]{1,0:T(8,128)}) custom-call(bf16[160,2048]{1,0:T(8,128)(2,1)S(1)} %get-tuple-element.14.gt_ref, bf16[160,6144]{1,0:T(8,128)(2,1)S(1)} %get-tuple-element.15.wt_ref, bf16[512,6144]{1,0:T(8,128)(2,1)S(1)} %get-tuple-element.16.hg_in, ...), custom_call_target="tpu_custom_call" | custom-call | tf_op jit(solution)/shard_map/pallas_call | solution.py:427

commit v6 on v5

--- a/solution.py
+++ b/solution.py
@@ -13,7 +13,7 @@
 COPY = 256
 LANES = 128
 SLAB = 256
-LAG = 2
+LAG = 3
 ROWS = 256
 EARLY = 2
 FLIGHT = 3

time: 60 us -> 59.3 us (0.988)
  Pallas kernels: 59.2 us -> 58.5 us
    pallas_call x1, Pallas kernels: 49.5 us -> 48.8 us  [device_step(): pl.pallas_call(functools.partial(first_kernel, tokens * n, n), out_shape=...]
where the time goes in v6:
time: 59.3 us; the launch traced here: 59.2 us
  Pallas kernels  58.5 us (99%)
  between operations  0.64 us (1%)
    pallas_call x1, Pallas kernels, device_step(): pl.pallas_call(functools.partial(first_kernel, tokens * n, n), out_shape=...  48.8 us
    pallas_call x1, Pallas kernels, device_step(): pl.pallas_call(functools.partial(second_kernel, blocks), out_shape=(jax.S...  9.75 us

profile of v6, /device:TPU:0, one launch (start us, length us, event | category | flops | bytes accessed | tf_op | source)
XLA Modules:
  0.0 59.2 jit_solution(4987765767807661496)
XLA Ops:
  0.6 48.8 %shard_map.75 = (bf16[160,2048]{1,0:T(8,128)(2,1)S(1)}, f32[8,2048]{1,0:T(8,128)S(1)}, f32[8,128]{1,0:T(8,128)S(1)}, f32[24,160,256]{2,1,0:T(8,128)S(1)}, bf16[1...) custom-call(bf16[2048,6144]{1,0:T(8,128)(2,1)} %hid_hbm.1, bf16[160,6144]{1,0:T(8,128)(2,1)} %bitcast.7, ...), custom_call_target="tpu_custom_call" | custom-call | tf_op jit(solution)/shard_map/pallas_call | solution.py:394
  49.4 9.8 %shard_map.76 = (bf16[2048,6144]{1,0:T(8,128)(2,1)}, f32[8,2048]{1,0:T(8,128)}, f32[1,128]{1,0:T(1,128)}, f32[160,6144]{1,0:T(8,128)}) custom-call(bf16[160,2048]{1,0:T(8,128)(2,1)S(1)} %get-tuple-element.14.gt_ref, bf16[160,6144]{1,0:T(8,128)(2,1)S(1)} %get-tuple-element.15.wt_ref, bf16[512,6144]{1,0:T(8,128)(2,1)S(1)} %get-tuple-element.16.hg_in, ...), custom_call_target="tpu_custom_call" | custom-call | tf_op jit(solution)/shard_map/pallas_call | solution.py:427
